TPU v7x, 128 devices: a whole 4x4x4 slice. The times are simulated.
128 devices in a mesh: fsdp: 8 (over z_lo, x), tp: 16 (over y, z_hi, core).
Axes of the slice: x: 4, y: 4, z: 4 (z_hi: 2, z_lo: 2; z = z_hi * 2 + z_lo), core: 2. Of those that a mesh axis runs over, the one named last changes fastest.
Arguments:
- ref_gate: bfloat16 [6144, 11008], P('fsdp', 'tp'), may hold values from -6 to 6
- ref_up: bfloat16 [6144, 11008], P('fsdp', 'tp'), may hold values from -6 to 6
- ref_residual: bfloat16 [6144, 4096], P('fsdp', 'tp'), may hold values from -6 to 6
- ref_modality: int32 [6144], P('fsdp'), may hold values 0 or 1
- ref_down_text: bfloat16 [4096, 11008], P('fsdp', 'tp'), may hold values from -0.0546875 to 0.0546875
- ref_down_image: bfloat16 [4096, 11008], P('fsdp', 'tp'), may hold values from -0.0546875 to 0.0546875
- pol_gate: bfloat16 [6144, 11008], P('fsdp', 'tp'), may hold values from -6 to 6
- pol_up: bfloat16 [6144, 11008], P('fsdp', 'tp'), may hold values from -6 to 6
- pol_modality: int32 [6144], P('fsdp'), may hold values 0 or 1
- pol_segment: int32 [6144], P('fsdp'), may hold values from 0 to 11, never falling along the last dimension, each value on 1 to 768 neighbouring positions
- pair_margin: float32 [6], replicated, may hold values from -30 to 30
- token_cotangent: bfloat16 [6144, 4096], P('fsdp', 'tp'), may hold values from -24 to 24
- pol_down_text: bfloat16 [4096, 11008], P('fsdp', 'tp'), may hold values from -0.0546875 to 0.0546875
- pol_down_image: bfloat16 [4096, 11008], P('fsdp', 'tp'), may hold values from -0.0546875 to 0.0546875
Outputs:
- ref_out: bfloat16 [6144, 4096], P('fsdp', 'tp')
- grad_gate: bfloat16 [6144, 11008], P('fsdp', 'tp')
- grad_up: bfloat16 [6144, 11008], P('fsdp', 'tp')
- grad_down_text: float32 [4096, 11008], P('fsdp', 'tp')
- grad_down_image: float32 [4096, 11008], P('fsdp', 'tp')
Inputs may be any that keep to these rules, and one draw needn't show every extreme that they name: `ref_modality`: 0 marks a text token, 1 an image token. `pol_modality`: 0 marks a text token, 1 an image token. `pol_segment`: response numbers never fall along the tokens; responses 2p and 2p + 1 are the chosen and the rejected response of pair p; every response has at least one token.
All inputs are finite; a program needn't handle non-finite values. No bound on the sum of `ref_modality` or of `pol_modality` on one device may be relied on, other than what follows from the above.
Results may differ from a plain program's by a relative error of at most 0.015.
Values may be sent and summed in bfloat16 or wider, within the bound.
No kernel may reach another device: no remote copies, remote signals or barrier semaphores. Data moves between devices by JAX's collectives and lax.ppermute only.
A program may use at most 128 MiB of HBM per device.

v0:
```python
import jax
import jax.numpy as jnp
from jax import lax
from jax.sharding import PartitionSpec as P

dpo_beta = 0.1


def sent_together(arrays, axis, dim, along):
    ends, at = ([], 0)
    for a in arrays[:-1]:
        at += a.shape[along]
        ends.append(at)
    both = jnp.concatenate(arrays, axis=along)
    return tuple(jnp.split(lax.all_gather(both, axis, axis=dim, tiled=True), ends, axis=along))


def split_hidden(gate, up, modality):
    gate_f = gate.astype(jnp.float32)
    up_f = up.astype(jnp.float32)
    sig = jax.nn.sigmoid(gate_f)
    act = gate_f * sig
    hidden = (act * up_f).astype(jnp.bfloat16)
    image = (modality == 1)[:, None]
    zero = jnp.zeros_like(hidden)
    return (jnp.where(image, zero, hidden), jnp.where(image, hidden, zero), gate_f, up_f, sig, act)


def forward_term(left_text, left_image, right_text, right_image):
    contract = (((1,), (1,)), ((), ()))
    part = lax.dot_general(left_text, right_text, contract, preferred_element_type=jnp.float32)
    return part + lax.dot_general(
        left_image, right_image, contract, preferred_element_type=jnp.float32
    )


def backward_term(left_text, left_image, right_text, right_image):
    part = jnp.dot(left_text, right_text, preferred_element_type=jnp.float32)
    return part + jnp.dot(left_image, right_image, preferred_element_type=jnp.float32)


def per_device(
    ref_gate,
    ref_up,
    ref_residual,
    ref_modality,
    ref_down_text,
    ref_down_image,
    pol_gate,
    pol_up,
    pol_modality,
    pol_segment,
    pair_margin,
    token_cotangent,
    pol_down_text,
    pol_down_image,
):
    ref_text, ref_image, _, _, _, _ = split_hidden(ref_gate, ref_up, ref_modality)
    pol_text, pol_image, gate_f, up_f, sig, act = split_hidden(pol_gate, pol_up, pol_modality)
    seg_ids = jnp.arange(2 * pair_margin.shape[0], dtype=jnp.int32)
    pair_weight = dpo_beta * jax.nn.sigmoid(-dpo_beta * pair_margin)
    table = jnp.repeat(pair_weight, 2) * jnp.where(seg_ids % 2 == 0, -1.0, 1.0).astype(jnp.float32)
    coef = jnp.sum(
        jnp.where(pol_segment[:, None] == seg_ids[None, :], table[None, :], jnp.float32(0.0)),
        axis=1,
    )
    local_cot = (coef[:, None] * token_cotangent.astype(jnp.float32)).astype(jnp.bfloat16)
    full_cot = lax.all_gather(local_cot, "tp", axis=1, tiled=True)
    image_p = (pol_modality == 1)[:, None]
    zero_cot = jnp.zeros_like(full_cot)
    cot_text = jnp.where(image_p, zero_cot, full_cot)
    cot_image = jnp.where(image_p, full_cot, zero_cot)
    whole_rt, whole_ri, whole_pt, whole_pi = sent_together(
        (ref_down_text, ref_down_image, pol_down_text, pol_down_image), "fsdp", 0, 1
    )
    terms = forward_term(ref_text, ref_image, whole_rt, whole_ri)
    d_hidden = backward_term(cot_text, cot_image, whole_pt, whole_pi)
    summed = lax.psum_scatter(
        terms.astype(jnp.bfloat16), "tp", scatter_dimension=1, tiled=True
    ).astype(jnp.float32)
    ref_out = (summed + ref_residual.astype(jnp.float32)).astype(jnp.bfloat16)
    grad_gate = (d_hidden * up_f * sig * (1.0 + gate_f * (1.0 - sig))).astype(jnp.bfloat16)
    grad_up = (d_hidden * act).astype(jnp.bfloat16)
    width = pol_down_text.shape[1]
    over_rows = (((0,), (0,)), ((), ()))
    term_text = lax.dot_general(cot_text, pol_text, over_rows, preferred_element_type=jnp.float32)
    term_image = lax.dot_general(
        cot_image, pol_image, over_rows, preferred_element_type=jnp.float32
    )
    grads = lax.psum_scatter(
        jnp.concatenate([term_text, term_image], axis=1).astype(jnp.bfloat16),
        "fsdp",
        scatter_dimension=0,
        tiled=True,
    ).astype(jnp.float32)
    return (ref_out, grad_gate, grad_up, grads[:, :width], grads[:, width:])


def solution(mesh):
    in_specs = (
        P("fsdp", "tp"),
        P("fsdp", "tp"),
        P("fsdp", "tp"),
        P("fsdp"),
        P("fsdp", "tp"),
        P("fsdp", "tp"),
        P("fsdp", "tp"),
        P("fsdp", "tp"),
        P("fsdp"),
        P("fsdp"),
        P(),
        P("fsdp", "tp"),
        P("fsdp", "tp"),
        P("fsdp", "tp"),
    )
    out_specs = (
        P("fsdp", "tp"),
        P("fsdp", "tp"),
        P("fsdp", "tp"),
        P("fsdp", "tp"),
        P("fsdp", "tp"),
    )
    return jax.shard_map(
        per_device, mesh=mesh, in_specs=in_specs, out_specs=out_specs, check_vma=False
    )
```

profile of v0, /device:TPU:0, one launch (start us, length us, event | category | flops | bytes accessed | tf_op | source)
XLA Modules:
  0.0 529.0 jit_solution(288210245870872746)
XLA Ops:
  7.2 0.0 all-gather.5.cloned.1.call-start
  7.2 0.7 divide_multiply_fusion
  7.9 0.1 broadcast_in_dim.66
  7.9 0.1 reshape.33
  8.0 0.8 select_reduce_fusion
  8.8 1.9 multiply_convert_fusion.1
  10.7 0.0 all-gather.5.cloned.1.call-update
  10.8 0.0 all-gather.3.cloned.1.call-start
  10.8 3.0 pad_maximum_fusion.1
  13.8 0.0 copy-start.1
  13.8 0.0 copy-start.6
  13.8 0.0 copy-start.7
  13.8 0.0 all-gather.3.cloned.1.call-update
  13.9 0.0 reduce-scatter.5.cloned.1.call-start
  13.9 0.6 copy-done.1
  14.5 67.7 %all-gather.5.cloned.1.call-done = bf16[768,4096]{1,0:T(8,128)(2,1)} async-done(((bf16[768,256]{1,0:T(8,128)(2,1)}), bf16[768,4096]{1,0:T(8,128)(2,1)}) %all-gather.5.cloned.1.call-update) | async-done | bytes 6291472 | tf_op jit(solution)/shard_map/all_gather | solution.py:68
  82.2 0.0 copy-done.6
  82.2 0.0 copy-done.7
  82.2 0.0 copy-start.3
  82.2 8.2 %convolution_convert_fusion = bf16[4096,688]{0,1:T(8,128)(2,1)S(1)} fusion(bf16[768,4096]{1,0:T(8,128)(2,1)} %all-gather.5.cloned.1.call-done, pred[768]{0:T(1024)(128)(4,1)S(1)} %broadcast_compare_fusion, bf16[768,688]{0,1:T(8,128)(2,1)S(1)} %copy-done.6, bf16[768,688]{0,1:T(8,128)(2,1)S(1)} %copy-done.7), kind=kOutput, calls=%fused_computation.2 | convolution fusion | flops 4339240960 | bytes 14041856 | tf_op jit(solution)/shard_map/dot_general | solution.py:87
  90.4 0.0 copy-done.3
  90.4 5.3 %convolution_convert_fusion.1 = bf16[4096,688]{0,1:T(8,128)(2,1)S(1)} fusion(bf16[768,4096]{1,0:T(8,128)(2,1)S(1)} %copy-done.3, pred[768]{0:T(1024)(128)(4,1)S(1)} %broadcast_compare_fusion, bf16[768,688]{0,1:T(8,128)(2,1)S(1)} %copy-done.6, bf16[768,688]{0,1:T(8,128)(2,1)S(1)} %copy-done.7), kind=kOutput, calls=%fused_computation.3 | convolution fusion | flops 4339240960 | bytes 14041856 | tf_op jit(solution)/shard_map/dot_general | solution.py:86
  95.7 10.4 %pad_maximum_fusion = bf16[4096,1376]{0,1:T(8,128)(2,1)} fusion(bf16[4096,688]{0,1:T(8,128)(2,1)S(1)} %convolution_convert_fusion, bf16[4096,688]{0,1:T(8,128)(2,1)S(1)} %convolution_convert_fusion.1), kind=kLoop, calls=%fused_computation.1 | loop fusion | flops 22544384 | bytes 22544384 | tf_op jit(solution)/shard_map/concatenate | solution.py:91
  106.1 0.0 copy-start.4
  106.2 0.0 copy-start.5
  106.2 0.0 reduce-scatter.5.cloned.1.call-update
  106.2 0.2 reduce-scatter.3.cloned.1.call-start
  106.4 0.4 copy-done.2
  106.8 200.0 %all-gather.3.cloned.1.call-done = bf16[4096,2752]{0,1:T(8,128)(2,1)} async-done(((bf16[512,2752]{0,1:T(8,128)(2,1)}), bf16[4096,2752]{0,1:T(8,128)(2,1)}) %all-gather.3.cloned.1.call-update) | async-done | bytes 22544400 | tf_op jit(solution)/shard_map/all_gather | solution.py:15
  306.8 0.0 copy-done.4
  306.8 0.0 copy-done.5
  306.8 7.6 %fusion.5 = f32[768,4096]{1,0:T(8,128)S(1)} fusion(bf16[4096,2752]{0,1:T(8,128)(2,1)} %all-gather.3.cloned.1.call-done, pred[768]{0:T(1024)(128)(4,1)S(1)} %broadcast_compare_fusion.1, bf16[768,688]{0,1:T(8,128)(2,1)S(1)} %copy-done.4, bf16[768,688]{0,1:T(8,128)(2,1)S(1)} %copy-done.5), kind=kOutput, calls=%fused_computation.11 | convolution fusion | flops 4333277184 | bytes 20333312 | tf_op jit(solution)/shard_map/dot_general | solution.py:31
  314.4 10.6 %add_convert_fusion = bf16[768,4096]{1,0:T(8,128)(2,1)} fusion(f32[768,4096]{1,0:T(8,128)S(1)} %fusion.5, bf16[4096,2752]{0,1:T(8,128)(2,1)} %all-gather.3.cloned.1.call-done, pred[768]{0:T(1024)(128)(4,1)S(1)} %broadcast_compare_fusion.1, bf16[768,688]{0,1:T(8,128)(2,1)S(1)} %copy-done.4, bf16[768,688]{0,1:T(8,128)(2,1)S(1)} %copy-done.5), kind=kOutput, calls=%fused_computation | convolution fusion | flops 4339568640 | bytes 26624768 | tf_op jit(solution)/shard_map/dot_general | solution.py:32
  325.1 0.0 reduce-scatter.3.cloned.1.call-update
  325.1 102.9 %reduce-scatter.5.cloned.1.call-done = bf16[512,1376]{0,1:T(8,128)(2,1)} async-done(((bf16[4096,1376]{0,1:T(8,128)(2,1)}), bf16[512,1376]{0,1:T(8,128)(2,1)}) %reduce-scatter.5.cloned.1.call-update) | async-done | bytes 1409040 | tf_op jit(solution)/shard_map/reduce_scatter | solution.py:90
  428.0 0.0 slice-start
  428.0 3.4 fusion.46
  431.4 0.0 slice-start.1
  431.4 0.0 copy-start.8
  431.4 8.8 %fusion = f32[768,688]{0,1:T(8,128)S(1)} fusion(bf16[4096,2752]{0,1:T(8,128)(2,1)} %all-gather.3.cloned.1.call-done, bf16[768,4096]{1,0:T(8,128)(2,1)} %all-gather.5.cloned.1.call-done, pred[768]{0:T(1024)(128)(4,1)S(1)} %broadcast_compare_fusion), kind=kOutput, calls=%fused_computation.6 | convolution fusion | flops 4331667456 | bytes 14041856 | tf_op jit(solution)/shard_map/dot_general | solution.py:39
  440.2 0.0 slice-done
  440.2 0.0 slice-done.1
  440.2 0.0 copy-done.8
  440.2 0.0 copy-start
  440.3 9.8 %multiply_convert_fusion = (bf16[768,688]{0,1:T(8,128)(2,1)}, bf16[768,688]{0,1:T(8,128)(2,1)}) fusion(bf16[768,688]{0,1:T(8,128)(2,1)S(1)} %copy-done.8, bf16[768,688]{0,1:T(8,128)(2,1)S(1)} %copy-done.6, f32[768,688]{0,1:T(8,128)S(1)} %fusion, bf16[4096,2752]{0,1:T(8,128)(2,1)} %all-gather.3.cloned.1.call-done, bf16[768,4096]{1,0:T(8,128)(2,1)S(1)} %bitcast.1, ...), kind=kOutput, calls=%fused_computation.33 | convolution fusion | flops 4340121600 | bytes 18268928 | tf_op jit(solution)/shard_map/dot_general | solution.py:38
  450.0 70.6 %reduce-scatter.3.cloned.1.call-done = bf16[768,256]{1,0:T(8,128)(2,1)} async-done(((bf16[768,4096]{1,0:T(8,128)(2,1)}), bf16[768,256]{1,0:T(8,128)(2,1)}) %reduce-scatter.3.cloned.1.call-update) | async-done | bytes 393232 | tf_op jit(solution)/shard_map/reduce_scatter | solution.py:78
  520.6 0.0 copy-done
  520.6 1.8 add_convert_fusion.1
  (5 shorter events, 0.0 us)
Async XLA Ops:
  7.2 75.0 %all-gather.5.cloned.1.call-start = ((), (), s32[]{:S(2)}) async-start(), calls=%async_computation.4 | async-start | bytes 6684672 | tf_op jit(solution)/shard_map/all_gather | solution.py:68
  10.8 296.1 %all-gather.3.cloned.1.call-start = ((), (), s32[]{:S(2)}) async-start(), calls=%async_computation.2 | async-start | bytes 25362432 | tf_op jit(solution)/shard_map/all_gather | solution.py:15
  13.8 0.7 copy-start.1
  13.8 68.4 %copy-start.6 = (bf16[768,688]{0,1:T(8,128)(2,1)S(1)}, bf16[768,688]{0,1:T(8,128)(2,1)}, u32[]{:S(2)}) copy-start(bf16[768,688]{0,1:T(8,128)(2,1)} %param.21) | copy-start | bytes 3170308
  13.8 68.4 %copy-start.7 = (bf16[768,688]{0,1:T(8,128)(2,1)S(1)}, bf16[768,688]{0,1:T(8,128)(2,1)}, u32[]{:S(2)}) copy-start(bf16[768,688]{0,1:T(8,128)(2,1)} %param.20) | copy-start | bytes 3170308
  13.9 414.1 %reduce-scatter.5.cloned.1.call-start = ((), (), s32[]{:S(2)}) async-start(), calls=%async_computation.5 | async-start | bytes 12681216 | tf_op jit(solution)/shard_map/reduce_scatter | solution.py:90
  82.2 8.2 %copy-start.3 = (bf16[768,4096]{1,0:T(8,128)(2,1)S(1)}, bf16[768,4096]{1,0:T(8,128)(2,1)}, u32[]{:S(2)}) copy-start(bf16[768,4096]{1,0:T(8,128)(2,1)} %all-gather.5.cloned.1.call-done) | copy-start | bytes 18874372
  106.1 0.7 copy-start.2
  106.1 200.7 %copy-start.4 = (bf16[768,688]{0,1:T(8,128)(2,1)S(1)}, bf16[768,688]{0,1:T(8,128)(2,1)}, u32[]{:S(2)}) copy-start(bf16[768,688]{0,1:T(8,128)(2,1)} %param.15) | copy-start | bytes 3170308
  106.2 200.7 %copy-start.5 = (bf16[768,688]{0,1:T(8,128)(2,1)S(1)}, bf16[768,688]{0,1:T(8,128)(2,1)}, u32[]{:S(2)}) copy-start(bf16[768,688]{0,1:T(8,128)(2,1)} %param.14) | copy-start | bytes 3170308
  106.2 414.4 %reduce-scatter.3.cloned.1.call-start = ((), (), s32[]{:S(2)}) async-start(), calls=%async_computation.3 | async-start | bytes 6684672 | tf_op jit(solution)/shard_map/reduce_scatter | solution.py:78
  428.0 12.2 %slice-start = ((s8[6291456]{0:T(1024)(128)(4,1)}), s8[4194304]{0:T(1024)(128)(4,1)S(1)}, s32[]{:S(2)}) async-start(s8[6291456]{0:T(1024)(128)(4,1)} %bitcast), calls=%async_computation.6 | async-start | bytes 8388608
  431.4 8.8 %slice-start.1 = ((s8[6291456]{0:T(1024)(128)(4,1)}), s8[2097152]{0:T(1024)(128)(4,1)S(1)}, s32[]{:S(2)}) async-start(s8[6291456]{0:T(1024)(128)(4,1)} %bitcast), calls=%async_computation.7 | async-start | bytes 4194304
  431.4 8.8 %copy-start.8 = (bf16[768,688]{0,1:T(8,128)(2,1)S(1)}, bf16[768,688]{0,1:T(8,128)(2,1)}, u32[]{:S(2)}) copy-start(bf16[768,688]{0,1:T(8,128)(2,1)} %param.20) | copy-start | bytes 3170308
  440.2 80.4 %copy-start = (bf16[768,256]{1,0:T(8,128)(2,1)S(1)}, bf16[768,256]{1,0:T(8,128)(2,1)}, u32[]{:S(2)}) copy-start(bf16[768,256]{1,0:T(8,128)(2,1)} %param.16) | copy-start | bytes 1179652
Sparse Core Ops, SparseCore 0:
  10.9 71.2 all-gather.4
  83.9 222.9 all-gather.2
  309.2 118.6 reduce-scatter.4
  432.0 88.5 reduce-scatter.2
where the time goes:
time: 529 us
  waiting for transfers between devices  441 us (83%)
  matrix products  50.3 us (10%)
  other arithmetic  18.6 us (4%)
  between operations  13.9 us (3%)
    all_gather x1, waiting for transfers between devices, sent_together(): lax.all_gather(both, axis, axis=dim, tiled=True)  200 us
    reduce_scatter x1, waiting for transfers between devices, per_device(): lax.psum_scatter(jnp.concatenate([term_text, term_image], axis=1).astype(...  103 us
    reduce_scatter x1, waiting for transfers between devices, per_device(): lax.psum_scatter(terms.astype(jnp.bfloat16), 'tp', scatter_dimension=1, t...  70.6 us
    all_gather x1, waiting for transfers between devices, per_device(): full_cot = lax.all_gather(local_cot, 'tp', axis=1, tiled=True)  67.7 us
    dot_general x1, matrix products, forward_term(): lax.dot_general(left_image, right_image, contract, preferred_element_type...  10.6 us
  transfers between devices with their start and end apart: 4, of which 4 were waited for; matrix products, arithmetic and copies ran while one was open for 13% of the time, Pallas kernels for 0%

commit v1 on v0

--- a/solution.py
+++ b/solution.py
@@ -65,7 +65,9 @@
         axis=1,
     )
     local_cot = (coef[:, None] * token_cotangent.astype(jnp.float32)).astype(jnp.bfloat16)
-    full_cot = lax.all_gather(local_cot, "tp", axis=1, tiled=True)
+    full_cot = jnp.concatenate(
+        lax.all_to_all(jnp.stack([local_cot] * lax.axis_size("tp")), "tp", 0, 0), axis=1
+    )
     image_p = (pol_modality == 1)[:, None]
     zero_cot = jnp.zeros_like(full_cot)
     cot_text = jnp.where(image_p, zero_cot, full_cot)

time: 529 us -> 565 us (1.068)
  local copies, waits for them, and re-layouts: 4.63 us -> 17.5 us
  waiting for transfers between devices: 441 us -> 452 us
  starting transfers between devices: 0.34 us -> 8.48 us
    all_to_all x0 -> x1, waiting for transfers between devices: none -> 283 us  [per_device(): lax.all_to_all(jnp.stack([local_cot] * lax.axis_size('tp')), 'tp', 0, 0)]
    all_gather x1, waiting for transfers between devices: 200 us -> 0.01 us  [sent_together(): lax.all_gather(both, axis, axis=dim, tiled=True)]
    all_gather x1 -> x0, waiting for transfers between devices: 67.7 us -> none  [per_device(): full_cot = lax.all_gather(local_cot, 'tp', axis=1, tiled=True)]
    all_to_all x0 -> x1, local copies, waits for them, and re-layouts: none -> 8.67 us  [per_device(): lax.all_to_all(jnp.stack([local_cot] * lax.axis_size('tp')), 'tp', 0, 0)]
    all_to_all x0 -> x1, starting transfers between devices: none -> 8.18 us  [per_device(): lax.all_to_all(jnp.stack([local_cot] * lax.axis_size('tp')), 'tp', 0, 0)]
    select_n x0 -> x1, other arithmetic: none -> 6.19 us  [per_device(): cot_text = jnp.where(image_p, zero_cot, full_cot)]
  transfers between devices with their start and end apart: 4 -> 4, of which waited for: 4 -> 3; matrix products, arithmetic and copies ran while one was open for 13% -> 15% of each run, Pallas kernels for 0% -> 0%
where the time goes in v1:
time: 565 us
  waiting for transfers between devices  452 us (80%)
  matrix products  51.4 us (9%)
  other arithmetic  21.5 us (4%)
  local copies, waits for them, and re-layouts  17.5 us (3%)
  between operations  13.9 us (2%)
  starting transfers between devices  8.48 us (2%)
    all_to_all x1, waiting for transfers between devices, per_device(): lax.all_to_all(jnp.stack([local_cot] * lax.axis_size('tp')), 'tp', 0, 0)  283 us
    reduce_scatter x1, waiting for transfers between devices, per_device(): lax.psum_scatter(jnp.concatenate([term_text, term_image], axis=1).astype(...  97.6 us
    reduce_scatter x1, waiting for transfers between devices, per_device(): lax.psum_scatter(terms.astype(jnp.bfloat16), 'tp', scatter_dimension=1, t...  71.1 us
  transfers between devices with their start and end apart: 4, of which 3 were waited for; matrix products, arithmetic and copies ran while one was open for 15% of the time, Pallas kernels for 0%

profile of v1, /device:TPU:0, one launch (start us, length us, event | category | flops | bytes accessed | tf_op | source)
XLA Modules:
  0.0 564.7 jit_solution(8516244707783311369)
XLA Ops:
  7.2 0.0 all-gather.2.cloned.1.call-start
  7.2 3.0 pad_maximum_fusion.1
  10.2 0.0 copy-start.12
  10.2 0.0 copy-start.5
  10.2 0.0 all-gather.2.cloned.1.call-update
  10.3 0.6 copy-done.12
  10.9 0.1 broadcast_in_dim.66
  11.0 0.1 reshape.41
  11.1 0.0 copy-done.5
  11.1 0.1 select_reduce_fusion
  11.2 0.1 copy-done.1
  11.3 0.2 multiply_convert_fusion.1
  11.4 3.2 stack.2
  14.7 0.0 copy-start.3
  14.7 8.2 %all-to-all-start = ((bf16[16,768,256]{2,1,0:T(8,128)(2,1)}), bf16[16,768,256]{2,1,0:T(8,128)(2,1)}, u32[]{:S(2)}, u32[]{:S(2)}) async-start(bf16[16,768,256]{2,1,0:T(8,128)(2,1)} %stack.2), calls=%async_computation.1 | async-start | bytes 12582912 | tf_op jit(solution)/shard_map/all_to_all | solution.py:69
  22.9 0.0 reduce-scatter.5.cloned.1.call-start
  22.9 0.0 copy-done.3
  22.9 283.1 %all-to-all-done = bf16[16,768,256]{2,1,0:T(8,128)(2,1)} async-done(((bf16[16,768,256]{2,1,0:T(8,128)(2,1)}), bf16[16,768,256]{2,1,0:T(8,128)(2,1)}, u32[]{:S(2)}, u32[]{:S(2)}) %all-to-all-start) | async-done | bytes 6291488 | tf_op jit(solution)/shard_map/all_to_all | solution.py:69
  306.0 8.7 %copy.20 = bf16[16,768,256]{1,2,0:T(8,128)(2,1)} copy(bf16[16,768,256]{2,1,0:T(8,128)(2,1)} %all-to-all-done) | data formatting | bytes 12582912 | tf_op jit(solution)/shard_map/all_to_all | solution.py:69
  314.7 6.2 %bitcast_select_fusion.1 = (bf16[768,4096]{0,1:T(8,128)(2,1)S(1)}, bf16[768,4096]{0,1:T(8,128)(2,1)}) fusion(bf16[16,768,256]{1,2,0:T(8,128)(2,1)} %copy.20, pred[768]{0:T(1024)(128)(4,1)S(1)} %broadcast_compare_fusion), kind=kLoop, calls=%fused_computation.5 | loop fusion | flops 6291456 | bytes 18875136 | tf_op jit(solution)/shard_map/jit(_where)/select_n | solution.py:73
  320.9 0.0 copy-start
  320.9 0.0 copy-start.8
  320.9 10.3 %convolution_convert_fusion = bf16[4096,688]{0,1:T(8,128)(2,1)S(1)} fusion(bf16[768,4096]{0,1:T(8,128)(2,1)} %get-tuple-element.6, pred[768]{0:T(1024)(128)(4,1)S(1)} %broadcast_compare_fusion, bf16[768,688]{0,1:T(8,128)(2,1)} %param.21, bf16[768,688]{0,1:T(8,128)(2,1)} %param.20), kind=kOutput, calls=%fused_computation.2 | convolution fusion | flops 4336095232 | bytes 14041856 | tf_op jit(solution)/shard_map/dot_general | solution.py:89
  331.2 0.0 copy-done
  331.2 0.0 copy-done.8
  331.2 0.0 copy-done.10
  331.2 5.1 convolution_convert_fusion.1
  336.4 10.2 %pad_maximum_fusion = bf16[4096,1376]{0,1:T(8,128)(2,1)} fusion(bf16[4096,688]{0,1:T(8,128)(2,1)S(1)} %convolution_convert_fusion, bf16[4096,688]{0,1:T(8,128)(2,1)S(1)} %convolution_convert_fusion.1), kind=kLoop, calls=%fused_computation.1 | loop fusion | flops 22544384 | bytes 22544384 | tf_op jit(solution)/shard_map/concatenate | solution.py:93
  346.6 0.0 reduce-scatter.5.cloned.1.call-update
  346.6 0.2 reduce-scatter.3.cloned.1.call-start
  346.8 0.4 copy-done.4
  347.2 0.5 copy-done.6
  347.8 0.3 copy-done.7
  348.1 7.6 %fusion.5 = f32[768,4096]{1,0:T(8,128)S(1)} fusion(bf16[4096,2752]{0,1:T(8,128)(2,1)} %all-gather.2.cloned.1.call-done, pred[768]{0:T(1024)(128)(4,1)S(1)} %broadcast_compare_fusion.1, bf16[768,688]{0,1:T(8,128)(2,1)S(1)} %copy-done.6, bf16[768,688]{0,1:T(8,128)(2,1)S(1)} %copy-done.7), kind=kOutput, calls=%fused_computation.11 | convolution fusion | flops 4333277184 | bytes 20333312 | tf_op jit(solution)/shard_map/dot_general | solution.py:31
  355.7 10.2 %add_convert_fusion = bf16[768,4096]{1,0:T(8,128)(2,1)} fusion(f32[768,4096]{1,0:T(8,128)S(1)} %fusion.5, bf16[4096,2752]{0,1:T(8,128)(2,1)} %all-gather.2.cloned.1.call-done, pred[768]{0:T(1024)(128)(4,1)S(1)} %broadcast_compare_fusion.1, bf16[768,688]{0,1:T(8,128)(2,1)S(1)} %copy-done.6, bf16[768,688]{0,1:T(8,128)(2,1)S(1)} %copy-done.7), kind=kOutput, calls=%fused_computation | convolution fusion | flops 4339568640 | bytes 26624768 | tf_op jit(solution)/shard_map/dot_general | solution.py:32
  365.9 0.0 reduce-scatter.3.cloned.1.call-update
  365.9 97.6 %reduce-scatter.5.cloned.1.call-done = bf16[512,1376]{0,1:T(8,128)(2,1)} async-done(((bf16[4096,1376]{0,1:T(8,128)(2,1)}), bf16[512,1376]{0,1:T(8,128)(2,1)}) %reduce-scatter.5.cloned.1.call-update) | async-done | bytes 1409040 | tf_op jit(solution)/shard_map/reduce_scatter | solution.py:92
  463.5 3.4 fusion.44
  466.9 8.5 %fusion = f32[768,688]{0,1:T(8,128)S(1)} fusion(bf16[768,4096]{0,1:T(8,128)(2,1)} %get-tuple-element.6, bf16[4096,2752]{0,1:T(8,128)(2,1)} %all-gather.2.cloned.1.call-done), kind=kOutput, calls=%fused_computation.6 | convolution fusion | flops 4328521728 | bytes 14041088 | tf_op jit(solution)/shard_map/dot_general | solution.py:39
  475.5 0.0 slice-done
  475.5 0.0 slice-done.1
  475.5 0.0 copy-done.9
  475.5 0.0 copy-done.11
  475.5 0.0 copy-start.2
  475.5 9.7 %multiply_convert_fusion = (bf16[768,688]{0,1:T(8,128)(2,1)}, bf16[768,688]{0,1:T(8,128)(2,1)}) fusion(bf16[768,688]{0,1:T(8,128)(2,1)S(1)} %copy-done.11, bf16[768,688]{0,1:T(8,128)(2,1)S(1)} %copy-done.9, f32[768,688]{0,1:T(8,128)S(1)} %fusion, bf16[768,4096]{0,1:T(8,128)(2,1)S(1)} %bitcast.10, bf16[4096,2752]{0,1:T(8,128)(2,1)} %all-gather.2.cloned.1.call-done), kind=kOutput, calls=%fused_computation.33 | convolution fusion | flops 4336975872 | bytes 18268160 | tf_op jit(solution)/shard_map/dot_general | solution.py:38
  485.2 71.1 %reduce-scatter.3.cloned.1.call-done = bf16[768,256]{1,0:T(8,128)(2,1)} async-done(((bf16[768,4096]{1,0:T(8,128)(2,1)}), bf16[768,256]{1,0:T(8,128)(2,1)}) %reduce-scatter.3.cloned.1.call-update) | async-done | bytes 393232 | tf_op jit(solution)/shard_map/reduce_scatter | solution.py:80
  556.3 0.0 copy-done.2
  556.3 1.8 add_convert_fusion.1
  (15 shorter events, 0.0 us)
Async XLA Ops:
  7.2 340.1 %all-gather.2.cloned.1.call-start = ((), (), s32[]{:S(2)}) async-start(), calls=%async_computation.3 | async-start | bytes 25362432 | tf_op jit(solution)/shard_map/all_gather | solution.py:15
  10.2 0.7 copy-start.12
  10.2 0.8 copy-start.5
  10.2 1.0 copy-start.1
  14.7 8.2 %copy-start.3 = (s32[768]{0:T(1024)S(1)}, s32[768]{0:T(1024)}, u32[]{:S(2)}) copy-start(s32[768]{0:T(1024)} %param.22) | copy-start | bytes 9220
  14.7 291.3 %all-to-all-start = ((bf16[16,768,256]{2,1,0:T(8,128)(2,1)}), bf16[16,768,256]{2,1,0:T(8,128)(2,1)}, u32[]{:S(2)}, u32[]{:S(2)}) async-start(bf16[16,768,256]{2,1,0:T(8,128)(2,1)} %stack.2), calls=%async_computation.1 | async-start | bytes 12582912 | tf_op jit(solution)/shard_map/all_to_all | solution.py:69
  22.9 440.7 %reduce-scatter.5.cloned.1.call-start = ((), (), s32[]{:S(2)}) async-start(), calls=%async_computation.5 | async-start | bytes 12681216 | tf_op jit(solution)/shard_map/reduce_scatter | solution.py:92
  320.9 10.3 %copy-start = (bf16[768,4096]{0,1:T(8,128)(2,1)}, bf16[768,4096]{0,1:T(8,128)(2,1)S(1)}, u32[]{:S(2)}) copy-start(bf16[768,4096]{0,1:T(8,128)(2,1)S(1)} %get-tuple-element.5) | copy-start | bytes 18874372
  320.9 10.4 %copy-start.8 = (bf16[768,688]{0,1:T(8,128)(2,1)S(1)}, bf16[768,688]{0,1:T(8,128)(2,1)}, u32[]{:S(2)}) copy-start(bf16[768,688]{0,1:T(8,128)(2,1)} %param.21) | copy-start | bytes 3170308
  320.9 10.4 %copy-start.10 = (bf16[768,688]{0,1:T(8,128)(2,1)S(1)}, bf16[768,688]{0,1:T(8,128)(2,1)}, u32[]{:S(2)}) copy-start(bf16[768,688]{0,1:T(8,128)(2,1)} %param.20) | copy-start | bytes 3170308
  346.6 0.7 copy-start.4
  346.6 1.2 copy-start.6
  346.6 1.6 copy-start.7
  346.6 209.7 %reduce-scatter.3.cloned.1.call-start = ((), (), s32[]{:S(2)}) async-start(), calls=%async_computation.4 | async-start | bytes 6684672 | tf_op jit(solution)/shard_map/reduce_scatter | solution.py:80
  463.5 12.0 %slice-start = ((s8[6291456]{0:T(1024)(128)(4,1)}), s8[4194304]{0:T(1024)(128)(4,1)S(1)}, s32[]{:S(2)}) async-start(s8[6291456]{0:T(1024)(128)(4,1)} %bitcast.9), calls=%async_computation.6 | async-start | bytes 8388608
  466.9 8.6 %slice-start.1 = ((s8[6291456]{0:T(1024)(128)(4,1)}), s8[2097152]{0:T(1024)(128)(4,1)S(1)}, s32[]{:S(2)}) async-start(s8[6291456]{0:T(1024)(128)(4,1)} %bitcast.9), calls=%async_computation.7 | async-start | bytes 4194304
  466.9 8.6 %copy-start.9 = (bf16[768,688]{0,1:T(8,128)(2,1)S(1)}, bf16[768,688]{0,1:T(8,128)(2,1)}, u32[]{:S(2)}) copy-start(bf16[768,688]{0,1:T(8,128)(2,1)} %param.21) | copy-start | bytes 3170308
  466.9 8.6 %copy-start.11 = (bf16[768,688]{0,1:T(8,128)(2,1)S(1)}, bf16[768,688]{0,1:T(8,128)(2,1)}, u32[]{:S(2)}) copy-start(bf16[768,688]{0,1:T(8,128)(2,1)} %param.20) | copy-start | bytes 3170308
  475.5 80.8 %copy-start.2 = (bf16[768,256]{1,0:T(8,128)(2,1)S(1)}, bf16[768,256]{1,0:T(8,128)(2,1)}, u32[]{:S(2)}) copy-start(bf16[768,256]{1,0:T(8,128)(2,1)} %param.16) | copy-start | bytes 1179652
Sparse Core Ops, SparseCore 0:
  10.4 277.7 all-gather.1
  346.7 116.7 reduce-scatter.4
  467.7 88.5 reduce-scatter.2
